TPU v7x, 512 devices: a whole 4x4x16 slice. The times are simulated.
512 devices in a mesh: section: 16 (over z), dp: 32 (over y, x, core).
Axes of the slice: x: 4, y: 4, z: 16, core: 2. Of those that a mesh axis runs over, the one named last changes fastest.
Arguments:
- acts: bfloat16 [16, 4, 32, 12, 16, 512], P('section', None, 'dp'), may hold values from -6 to 6
- out_grad: bfloat16 [4, 32, 12, 16, 512], P(None, 'dp'), may hold values from -6 to 6
- depth_kernel: bfloat16 [16, 3, 3, 512], P('section'), may hold values from -2 to 2
- point_weight: bfloat16 [16, 512, 512], P('section'), may hold values from -0.25 to 0.25
- bn_gain: float32 [16, 512], P('section'), may hold values from 0.15 to 0.45
Outputs:
- act_grad: bfloat16 [16, 4, 32, 12, 16, 512], P('section', None, 'dp')
- point_grad: float32 [16, 512, 512], P('section')
- kernel_grad: float32 [16, 3, 3, 512], P('section')
- gain_grad: float32 [16, 512], P('section')
- bias_grad: float32 [16, 512], P('section')
All inputs are finite; a program needn't handle non-finite values.
Results may differ from a plain program's by a relative error of at most 0.025.
Values may be sent and summed in bfloat16 or wider, within the bound.
A program may use at most 64 MiB of HBM per device.

v0:
```python
import jax
import jax.numpy as jnp
from jax import lax
from jax.sharding import PartitionSpec as P

epsilon = 1e-05


def from_everyone(x, axis):
    copies = jnp.broadcast_to(x, (lax.axis_size(axis), *x.shape))
    return lax.all_to_all(copies, axis, split_axis=0, concat_axis=0, tiled=True)


def taken_together(x, axis):
    everything = from_everyone(x, axis)
    return jnp.sum(everything, axis=0)


def in_one(arrays, axis):
    ravelled, at, finished = (jnp.concatenate([a.reshape(-1) for a in arrays]), 0, [])
    running = taken_together(ravelled, axis)
    for a in arrays:
        finished.append(running[at : at + a.size].reshape(a.shape))
        at += a.size
    return tuple(finished)


def shifted(x, axis, by):
    length = lax.axis_size(axis)
    pairs = [(i, i + by) for i in range(length) if 0 <= i + by < length]
    return lax.ppermute(x, axis, pairs)


def depthwise(active, kernel):
    padded = jnp.pad(active, ((0, 0), (1, 1), (1, 1), (0, 0)))
    height, width = (active.shape[1], active.shape[2])
    summed = jnp.zeros(active.shape, jnp.float32)
    for row_off in range(3):
        for col_off in range(3):
            summed = (
                summed
                + kernel[row_off, col_off]
                * padded[:, row_off : row_off + height, col_off : col_off + width]
            )
    return summed


def depthwise_back(grad, kernel):
    padded = jnp.pad(grad, ((0, 0), (1, 1), (1, 1), (0, 0)))
    height, width = (grad.shape[1], grad.shape[2])
    summed = jnp.zeros(grad.shape, jnp.float32)
    for row_off in range(3):
        for col_off in range(3):
            summed = (
                summed
                + kernel[row_off, col_off]
                * padded[:, 2 - row_off : 2 - row_off + height, 2 - col_off : 2 - col_off + width]
            )
    return summed


def kernel_terms(active, grad):
    padded = jnp.pad(active, ((0, 0), (1, 1), (1, 1), (0, 0)))
    height, width = (active.shape[1], active.shape[2])
    table = []
    for row_off in range(3):
        line = []
        for col_off in range(3):
            line.append(
                jnp.sum(
                    padded[:, row_off : row_off + height, col_off : col_off + width] * grad,
                    axis=(0, 1, 2),
                )
            )
        table.append(jnp.stack(line))
    return jnp.stack(table)


def pick(array, slot):
    return lax.dynamic_index_in_dim(array, slot, 0, keepdims=False)


def body(acts, out_grad, depth_kernel, point_weight, bn_gain):
    sections = lax.axis_size("section")
    replicas = lax.axis_size("dp")
    my_section = lax.axis_index("section")
    micros, images, height, width, channels = acts.shape[1:]
    rows = images * height * width
    count = images * replicas * height * width
    shape = (images, height, width, channels)
    inputs = acts[0]
    kernel = depth_kernel[0].astype(jnp.float32)
    weight = point_weight[0]
    gain = bn_gain[0]
    active = jnp.maximum(inputs.astype(jnp.float32), 0.0)
    depth_out = depthwise(active.reshape(micros * images, height, width, channels), kernel).astype(
        jnp.bfloat16
    )
    depth_flat = depth_out.reshape(micros * rows, channels)
    pre_norm = jnp.dot(depth_flat, weight, preferred_element_type=jnp.float32).reshape(
        micros, rows, channels
    )
    pre_bank = jnp.zeros((1,), jnp.bfloat16)
    depth_bank = jnp.zeros((1,), jnp.float32)
    depth_rows = depth_flat.reshape(micros, rows, channels)

    def step(turn, carry):
        incoming, grads_out, gain_acc, bias_acc, point_acc, kernel_acc, pre_store, depth_store = (
            carry
        )
        micro = turn - (sections - 1 - my_section)
        valid = jnp.logical_and(micro >= 0, micro < micros)
        slot = jnp.clip(micro, 0, micros - 1)
        flag = valid.astype(jnp.float32)
        upstream = jnp.where(my_section == sections - 1, pick(out_grad, slot), incoming)
        upstream = upstream.astype(jnp.float32).reshape(rows, channels)
        pre_slot = pick(pre_norm, slot)
        first, second, sum_grad, raw_cross = in_one(
            (
                jnp.sum(pre_slot, axis=0),
                jnp.sum(pre_slot * pre_slot, axis=0),
                jnp.sum(upstream, axis=0),
                jnp.sum(upstream * pre_slot, axis=0),
            ),
            "dp",
        )
        center = first / count
        inv_std = lax.rsqrt(second / count - center * center + epsilon)
        normed = (pre_slot - center) * inv_std
        sum_cross = inv_std * (raw_cross - center * sum_grad)
        pre_grad = (
            gain * inv_std * (upstream - sum_grad / count - normed * sum_cross / count)
        ).astype(jnp.bfloat16)
        depth_grad = lax.dot_general(
            pre_grad, weight, (((1,), (1,)), ((), ())), preferred_element_type=jnp.float32
        ).reshape(shape)
        active_slot = pick(active, slot)
        input_slot = pick(inputs, slot)
        back = depthwise_back(depth_grad, kernel)
        input_grad = (upstream.reshape(shape) + jnp.where(input_slot > 0, back, 0.0)).astype(
            jnp.bfloat16
        )
        gain_acc = gain_acc + flag * sum_cross
        bias_acc = bias_acc + flag * sum_grad
        depth_slot = pick(depth_rows, slot)
        point_acc = point_acc + flag * lax.dot_general(
            depth_slot, pre_grad, (((0,), (0,)), ((), ())), preferred_element_type=jnp.float32
        )
        kernel_acc = kernel_acc + flag * kernel_terms(active_slot, depth_grad)
        kept_grad = jnp.where(valid, input_grad, pick(grads_out, slot))
        grads_out = lax.dynamic_update_index_in_dim(grads_out, kept_grad, slot, 0)
        incoming = shifted(input_grad, "section", -1)
        return (
            incoming,
            grads_out,
            gain_acc,
            bias_acc,
            point_acc,
            kernel_acc,
            pre_store,
            depth_store,
        )

    start = (
        jnp.zeros(shape, jnp.bfloat16),
        jnp.zeros((micros,) + shape, jnp.bfloat16),
        jnp.zeros((channels,), jnp.float32),
        jnp.zeros((channels,), jnp.float32),
        jnp.zeros((channels, channels), jnp.float32),
        jnp.zeros((3, 3, channels), jnp.float32),
        pre_bank,
        depth_bank,
    )
    final = lax.fori_loop(0, sections + micros - 1, step, start)
    grads_out, gain_acc, bias_acc, point_acc, kernel_acc, pre_store, depth_store = final[1:]
    point_sum, kernel_sum = (
        lax.psum(point_acc.astype(jnp.bfloat16), "dp").astype(jnp.float32),
        lax.psum(kernel_acc.astype(jnp.bfloat16), "dp").astype(jnp.float32),
    )
    return (grads_out[None], point_sum[None], kernel_sum[None], gain_acc[None], bias_acc[None])


def solution(mesh):
    return jax.shard_map(
        body,
        mesh=mesh,
        in_specs=(
            P("section", None, "dp", None, None, None),
            P(None, "dp", None, None, None),
            P("section", None, None, None),
            P("section", None, None),
            P("section", None),
        ),
        out_specs=(
            P("section", None, "dp", None, None, None),
            P("section", None, None),
            P("section", None, None, None),
            P("section", None),
            P("section", None),
        ),
        check_vma=False,
    )
```

profile of v0, /device:TPU:1, one launch (start us, length us, event | category | flops | bytes accessed | tf_op | source)
XLA Modules:
  0.0 723.6 jit_solution(13232851758177793527)
XLA Ops:
  20.9 555.3 %while.26 = (s32[]{:T(128)}, bf16[1,12,16,512]{3,2,1,0:T(8,128)(2,1)S(1)}, bf16[4,1,12,16,512]{4,3,2,1,0:T(8,128)(2,1)}, f32[512]{0:T(512)S(1)}, f32[512]{0:T(51...) while((s32[]{:T(128)}, ...), condition=%wide.region_15.16_spmd.clone, body=%wide.region_0.15_spmd.clone.sunk | while | flops 208999424 | bytes 16183717 | solution.py:174
  23.9 10.4 %all-to-all-start = ((f32[32,1,2048]{2,1,0:T(1,128)}), f32[32,1,2048]{2,1,0:T(1,128)S(1)}, u32[]{:S(2)}, u32[]{:S(2)}) async-start(f32[32,1,2048]{2,1,0:T(1,128)} %broadcast_in_dim.88), calls=%async_computation | async-start | bytes 524288 | tf_op jit(solution)/shard_map/while/body/eval_jaxpr/all_to_all | solution.py:11
  64.2 7.0 all-to-all-done
  148.1 7.0 all-to-all-done
  161.0 7.0 collective-permute-done
  177.3 7.0 all-to-all-done
  190.2 7.0 collective-permute-done
  206.4 7.0 all-to-all-done
  219.3 7.0 collective-permute-done
  248.5 7.0 collective-permute-done
  264.7 7.0 all-to-all-done
  277.6 7.0 collective-permute-done
  306.8 7.0 collective-permute-done
  336.0 7.0 collective-permute-done
  365.1 7.0 collective-permute-done
  394.3 7.0 collective-permute-done
  423.4 7.0 collective-permute-done
  452.6 7.0 collective-permute-done
  481.7 7.0 collective-permute-done
  510.9 7.0 collective-permute-done
  540.0 7.0 collective-permute-done
  569.2 7.0 collective-permute-done
  577.1 120.4 %psum.15 = bf16[1,3,3,512]{3,0,2,1:T(2,128)(2,1)S(1)} all-reduce(bf16[1,3,3,512]{3,0,2,1:T(2,128)(2,1)S(1)} %broadcast_in_dim.78), channel_id=1, replica_groups=mesh['section'=16,'dp'=32] {'dp'}, use_global_device_ids=true, to_apply=%region_17.18 | all-reduce | flops 4608 | bytes 18432 | tf_op jit(solution)/shard_map/psum | solution.py:178
  698.1 16.5 %all-reduce.5.cloned.1.call-done = bf16[1,512,512]{2,1,0:T(8,128)(2,1)} async-done(((bf16[1,512,512]{2,1,0:T(8,128)(2,1)}), bf16[1,512,512]{2,1,0:T(8,128)(2,1)}) %all-reduce.5.cloned.1.call-update) | async-done | bytes 524304 | tf_op jit(solution)/shard_map/psum | solution.py:177
  (506 shorter events, 420.7 us)
Async XLA Ops:
  7.2 707.4 %all-reduce.5.cloned.1.call-start = ((), (), s32[]{:S(2)}) async-start(), calls=%async_computation.1 | async-start | bytes 1048576 | tf_op jit(solution)/shard_map/psum | solution.py:177
  23.9 19.4 %all-to-all-start = ((f32[32,1,2048]{2,1,0:T(1,128)}), f32[32,1,2048]{2,1,0:T(1,128)S(1)}, u32[]{:S(2)}, u32[]{:S(2)}) async-start(f32[32,1,2048]{2,1,0:T(1,128)} %broadcast_in_dim.88), calls=%async_computation | async-start | bytes 524288 | tf_op jit(solution)/shard_map/while/body/eval_jaxpr/all_to_all | solution.py:11
  57.7 13.5 %all-to-all-start = ((f32[32,1,2048]{2,1,0:T(1,128)}), f32[32,1,2048]{2,1,0:T(1,128)S(1)}, u32[]{:S(2)}, u32[]{:S(2)}) async-start(f32[32,1,2048]{2,1,0:T(1,128)} %broadcast_in_dim.88), calls=%async_computation | async-start | bytes 524288 | tf_op jit(solution)/shard_map/while/body/eval_jaxpr/all_to_all | solution.py:11
  85.6 13.5 %all-to-all-start = ((f32[32,1,2048]{2,1,0:T(1,128)}), f32[32,1,2048]{2,1,0:T(1,128)S(1)}, u32[]{:S(2)}, u32[]{:S(2)}) async-start(f32[32,1,2048]{2,1,0:T(1,128)} %broadcast_in_dim.88), calls=%async_computation | async-start | bytes 524288 | tf_op jit(solution)/shard_map/while/body/eval_jaxpr/all_to_all | solution.py:11
  113.6 13.5 %all-to-all-start = ((f32[32,1,2048]{2,1,0:T(1,128)}), f32[32,1,2048]{2,1,0:T(1,128)S(1)}, u32[]{:S(2)}, u32[]{:S(2)}) async-start(f32[32,1,2048]{2,1,0:T(1,128)} %broadcast_in_dim.88), calls=%async_computation | async-start | bytes 524288 | tf_op jit(solution)/shard_map/while/body/eval_jaxpr/all_to_all | solution.py:11
  141.6 13.5 %all-to-all-start = ((f32[32,1,2048]{2,1,0:T(1,128)}), f32[32,1,2048]{2,1,0:T(1,128)S(1)}, u32[]{:S(2)}, u32[]{:S(2)}) async-start(f32[32,1,2048]{2,1,0:T(1,128)} %broadcast_in_dim.88), calls=%async_computation | async-start | bytes 524288 | tf_op jit(solution)/shard_map/while/body/eval_jaxpr/all_to_all | solution.py:11
  158.2 9.8 %collective-permute-start = (bf16[1,12,16,512]{3,2,1,0:T(8,128)(2,1)S(1)}, bf16[1,12,16,512]{3,2,1,0:T(8,128)(2,1)S(1)}, u32[]{:S(2)}, u32[]{:S(2)}) collective-permute-start(bf16[1,12,16,512]{3,2,1,0:T(8,128)(2,1)S(1)} %get-tuple-element.682), channel_id=1, source_target_pairs={{32,0},{64,32},{96,64},{128,96},{160,128},{192,160},{224,192},{256... | collective-permute-start | bytes 589832 | tf_op jit(solution)/shard_map/while/body/eval_jaxpr/ppermute | solution.py:31
  171.0 13.2 %all-to-all-start = ((f32[32,1,2048]{2,1,0:T(1,128)}), f32[32,1,2048]{2,1,0:T(1,128)S(1)}, u32[]{:S(2)}, u32[]{:S(2)}) async-start(f32[32,1,2048]{2,1,0:T(1,128)} %broadcast_in_dim.88), calls=%async_computation | async-start | bytes 524288 | tf_op jit(solution)/shard_map/while/body/eval_jaxpr/all_to_all | solution.py:11
  187.3 9.8 %collective-permute-start = (bf16[1,12,16,512]{3,2,1,0:T(8,128)(2,1)S(1)}, bf16[1,12,16,512]{3,2,1,0:T(8,128)(2,1)S(1)}, u32[]{:S(2)}, u32[]{:S(2)}) collective-permute-start(bf16[1,12,16,512]{3,2,1,0:T(8,128)(2,1)S(1)} %get-tuple-element.682), channel_id=1, source_target_pairs={{32,0},{64,32},{96,64},{128,96},{160,128},{192,160},{224,192},{256... | collective-permute-start | bytes 589832 | tf_op jit(solution)/shard_map/while/body/eval_jaxpr/ppermute | solution.py:31
  200.2 13.2 %all-to-all-start = ((f32[32,1,2048]{2,1,0:T(1,128)}), f32[32,1,2048]{2,1,0:T(1,128)S(1)}, u32[]{:S(2)}, u32[]{:S(2)}) async-start(f32[32,1,2048]{2,1,0:T(1,128)} %broadcast_in_dim.88), calls=%async_computation | async-start | bytes 524288 | tf_op jit(solution)/shard_map/while/body/eval_jaxpr/all_to_all | solution.py:11
  229.3 13.2 %all-to-all-start = ((f32[32,1,2048]{2,1,0:T(1,128)}), f32[32,1,2048]{2,1,0:T(1,128)S(1)}, u32[]{:S(2)}, u32[]{:S(2)}) async-start(f32[32,1,2048]{2,1,0:T(1,128)} %broadcast_in_dim.88), calls=%async_computation | async-start | bytes 524288 | tf_op jit(solution)/shard_map/while/body/eval_jaxpr/all_to_all | solution.py:11
  258.5 13.2 %all-to-all-start = ((f32[32,1,2048]{2,1,0:T(1,128)}), f32[32,1,2048]{2,1,0:T(1,128)S(1)}, u32[]{:S(2)}, u32[]{:S(2)}) async-start(f32[32,1,2048]{2,1,0:T(1,128)} %broadcast_in_dim.88), calls=%async_computation | async-start | bytes 524288 | tf_op jit(solution)/shard_map/while/body/eval_jaxpr/all_to_all | solution.py:11
  274.8 9.8 %collective-permute-start = (bf16[1,12,16,512]{3,2,1,0:T(8,128)(2,1)S(1)}, bf16[1,12,16,512]{3,2,1,0:T(8,128)(2,1)S(1)}, u32[]{:S(2)}, u32[]{:S(2)}) collective-permute-start(bf16[1,12,16,512]{3,2,1,0:T(8,128)(2,1)S(1)} %get-tuple-element.682), channel_id=1, source_target_pairs={{32,0},{64,32},{96,64},{128,96},{160,128},{192,160},{224,192},{256... | collective-permute-start | bytes 589832 | tf_op jit(solution)/shard_map/while/body/eval_jaxpr/ppermute | solution.py:31
  287.6 13.2 %all-to-all-start = ((f32[32,1,2048]{2,1,0:T(1,128)}), f32[32,1,2048]{2,1,0:T(1,128)S(1)}, u32[]{:S(2)}, u32[]{:S(2)}) async-start(f32[32,1,2048]{2,1,0:T(1,128)} %broadcast_in_dim.88), calls=%async_computation | async-start | bytes 524288 | tf_op jit(solution)/shard_map/while/body/eval_jaxpr/all_to_all | solution.py:11
  304.0 9.8 %collective-permute-start = (bf16[1,12,16,512]{3,2,1,0:T(8,128)(2,1)S(1)}, bf16[1,12,16,512]{3,2,1,0:T(8,128)(2,1)S(1)}, u32[]{:S(2)}, u32[]{:S(2)}) collective-permute-start(bf16[1,12,16,512]{3,2,1,0:T(8,128)(2,1)S(1)} %get-tuple-element.682), channel_id=1, source_target_pairs={{32,0},{64,32},{96,64},{128,96},{160,128},{192,160},{224,192},{256... | collective-permute-start | bytes 589832 | tf_op jit(solution)/shard_map/while/body/eval_jaxpr/ppermute | solution.py:31
  316.8 13.2 %all-to-all-start = ((f32[32,1,2048]{2,1,0:T(1,128)}), f32[32,1,2048]{2,1,0:T(1,128)S(1)}, u32[]{:S(2)}, u32[]{:S(2)}) async-start(f32[32,1,2048]{2,1,0:T(1,128)} %broadcast_in_dim.88), calls=%async_computation | async-start | bytes 524288 | tf_op jit(solution)/shard_map/while/body/eval_jaxpr/all_to_all | solution.py:11
  345.9 13.2 %all-to-all-start = ((f32[32,1,2048]{2,1,0:T(1,128)}), f32[32,1,2048]{2,1,0:T(1,128)S(1)}, u32[]{:S(2)}, u32[]{:S(2)}) async-start(f32[32,1,2048]{2,1,0:T(1,128)} %broadcast_in_dim.88), calls=%async_computation | async-start | bytes 524288 | tf_op jit(solution)/shard_map/while/body/eval_jaxpr/all_to_all | solution.py:11
  375.1 13.2 %all-to-all-start = ((f32[32,1,2048]{2,1,0:T(1,128)}), f32[32,1,2048]{2,1,0:T(1,128)S(1)}, u32[]{:S(2)}, u32[]{:S(2)}) async-start(f32[32,1,2048]{2,1,0:T(1,128)} %broadcast_in_dim.88), calls=%async_computation | async-start | bytes 524288 | tf_op jit(solution)/shard_map/while/body/eval_jaxpr/all_to_all | solution.py:11
  404.2 13.2 %all-to-all-start = ((f32[32,1,2048]{2,1,0:T(1,128)}), f32[32,1,2048]{2,1,0:T(1,128)S(1)}, u32[]{:S(2)}, u32[]{:S(2)}) async-start(f32[32,1,2048]{2,1,0:T(1,128)} %broadcast_in_dim.88), calls=%async_computation | async-start | bytes 524288 | tf_op jit(solution)/shard_map/while/body/eval_jaxpr/all_to_all | solution.py:11
  433.4 13.2 %all-to-all-start = ((f32[32,1,2048]{2,1,0:T(1,128)}), f32[32,1,2048]{2,1,0:T(1,128)S(1)}, u32[]{:S(2)}, u32[]{:S(2)}) async-start(f32[32,1,2048]{2,1,0:T(1,128)} %broadcast_in_dim.88), calls=%async_computation | async-start | bytes 524288 | tf_op jit(solution)/shard_map/while/body/eval_jaxpr/all_to_all | solution.py:11
  462.6 13.2 %all-to-all-start = ((f32[32,1,2048]{2,1,0:T(1,128)}), f32[32,1,2048]{2,1,0:T(1,128)S(1)}, u32[]{:S(2)}, u32[]{:S(2)}) async-start(f32[32,1,2048]{2,1,0:T(1,128)} %broadcast_in_dim.88), calls=%async_computation | async-start | bytes 524288 | tf_op jit(solution)/shard_map/while/body/eval_jaxpr/all_to_all | solution.py:11
  491.7 13.2 %all-to-all-start = ((f32[32,1,2048]{2,1,0:T(1,128)}), f32[32,1,2048]{2,1,0:T(1,128)S(1)}, u32[]{:S(2)}, u32[]{:S(2)}) async-start(f32[32,1,2048]{2,1,0:T(1,128)} %broadcast_in_dim.88), calls=%async_computation | async-start | bytes 524288 | tf_op jit(solution)/shard_map/while/body/eval_jaxpr/all_to_all | solution.py:11
  520.9 13.2 %all-to-all-start = ((f32[32,1,2048]{2,1,0:T(1,128)}), f32[32,1,2048]{2,1,0:T(1,128)S(1)}, u32[]{:S(2)}, u32[]{:S(2)}) async-start(f32[32,1,2048]{2,1,0:T(1,128)} %broadcast_in_dim.88), calls=%async_computation | async-start | bytes 524288 | tf_op jit(solution)/shard_map/while/body/eval_jaxpr/all_to_all | solution.py:11
  550.0 13.2 %all-to-all-start = ((f32[32,1,2048]{2,1,0:T(1,128)}), f32[32,1,2048]{2,1,0:T(1,128)S(1)}, u32[]{:S(2)}, u32[]{:S(2)}) async-start(f32[32,1,2048]{2,1,0:T(1,128)} %broadcast_in_dim.88), calls=%async_computation | async-start | bytes 524288 | tf_op jit(solution)/shard_map/while/body/eval_jaxpr/all_to_all | solution.py:11
  (41 other events, 619.8 us)
Sparse Core Ops, SparseCore 0:
  577.2 137.3 all-reduce.4
where the time goes:
time: 729 us; the launch traced here: 724 us
  waiting for transfers between devices  275 us (38%)
  blocking collectives  120 us (16%)
  starting transfers between devices  115 us (16%)
  other arithmetic  108 us (15%)
  local copies, waits for them, and re-layouts  55.2 us (8%)
  matrix products  33.4 us (5%)
  between operations  14.1 us (2%)
    all_to_all x19, waiting for transfers between devices, from_everyone(): return lax.all_to_all(copies, axis, split_axis=0, concat_axis=0, tiled=True)  132 us
    ppermute x19, waiting for transfers between devices, shifted(): return lax.ppermute(x, axis, pairs)  127 us
    psum x1, blocking collectives, body(): lax.psum(kernel_acc.astype(jnp.bfloat16), 'dp').astype(jnp.float32)  120 us
    all_to_all x19, starting transfers between devices, from_everyone(): return lax.all_to_all(copies, axis, split_axis=0, concat_axis=0, tiled=True)  87.7 us
    dynamic_update_slice x19, other arithmetic, step(): grads_out = lax.dynamic_update_index_in_dim(grads_out, kept_grad, slot, 0)  37.7 us
    ppermute x19, starting transfers between devices, shifted(): return lax.ppermute(x, axis, pairs)  26.8 us
    dot_general x19, matrix products, step(): lax.dot_general(depth_slot, pre_grad, (((0,), (0,)), ((), ())), preferred...  25.6 us
    reduce_sum x19, other arithmetic, step(): jnp.sum(pre_slot, axis=0)  20 us
  transfers between devices with their start and end apart: 39, of which 39 were waited for; matrix products, arithmetic and copies ran while one was open for 9% of the time, Pallas kernels for 0%

commit v1 on v0

--- a/solution.py
+++ b/solution.py
@@ -175,7 +175,7 @@
     grads_out, gain_acc, bias_acc, point_acc, kernel_acc, pre_store, depth_store = final[1:]
     point_sum, kernel_sum = (
         lax.psum(point_acc.astype(jnp.bfloat16), "dp").astype(jnp.float32),
-        lax.psum(kernel_acc.astype(jnp.bfloat16), "dp").astype(jnp.float32),
+        jnp.sum(lax.all_gather(kernel_acc.astype(jnp.bfloat16), "dp"), axis=0).astype(jnp.float32),
     )
     return (grads_out[None], point_sum[None], kernel_sum[None], gain_acc[None], bias_acc[None])
 

time: 729 us -> 729 us (level)
  waiting for transfers between devices: 275 us -> 372 us
  blocking collectives: 120 us -> 23.8 us
    psum x1 -> x0, blocking collectives: 120 us -> none  [body(): lax.psum(kernel_acc.astype(jnp.bfloat16), 'dp').astype(jnp.float32)]
    psum x1, waiting for transfers between devices: 16.5 us -> 113 us  [body(): lax.psum(point_acc.astype(jnp.bfloat16), 'dp').astype(jnp.float32)]
    all_gather x0 -> x1, blocking collectives: none -> 23.8 us  [body(): lax.all_gather(kernel_acc.astype(jnp.bfloat16), 'dp')]
where the time goes in v1:
time: 729 us; the launch traced here: 724 us
  waiting for transfers between devices  372 us (51%)
  starting transfers between devices  115 us (16%)
  other arithmetic  108 us (15%)
  local copies, waits for them, and re-layouts  55.8 us (8%)
  matrix products  33.4 us (5%)
  blocking collectives  23.8 us (3%)
  between operations  14.1 us (2%)
    all_to_all x19, waiting for transfers between devices, from_everyone(): return lax.all_to_all(copies, axis, split_axis=0, concat_axis=0, tiled=True)  132 us
    ppermute x19, waiting for transfers between devices, shifted(): return lax.ppermute(x, axis, pairs)  127 us
    psum x1, waiting for transfers between devices, body(): lax.psum(point_acc.astype(jnp.bfloat16), 'dp').astype(jnp.float32)  113 us
    all_to_all x19, starting transfers between devices, from_everyone(): return lax.all_to_all(copies, axis, split_axis=0, concat_axis=0, tiled=True)  87.7 us
    dynamic_update_slice x19, other arithmetic, step(): grads_out = lax.dynamic_update_index_in_dim(grads_out, kept_grad, slot, 0)  37.7 us
    ppermute x19, starting transfers between devices, shifted(): return lax.ppermute(x, axis, pairs)  26.8 us
    dot_general x19, matrix products, step(): lax.dot_general(depth_slot, pre_grad, (((0,), (0,)), ((), ())), preferred...  25.6 us
    all_gather x1, blocking collectives, body(): lax.all_gather(kernel_acc.astype(jnp.bfloat16), 'dp')  23.8 us
  transfers between devices with their start and end apart: 39, of which 39 were waited for; matrix products, arithmetic and copies ran while one was open for 9% of the time, Pallas kernels for 0%

profile of v1, /device:TPU:1, one launch (start us, length us, event | category | flops | bytes accessed | tf_op | source)
XLA Modules:
  0.0 723.6 jit_solution(8096581368497140395)
XLA Ops:
  20.9 555.3 %while.26 = (s32[]{:T(128)}, bf16[1,12,16,512]{3,2,1,0:T(8,128)(2,1)S(1)}, bf16[4,1,12,16,512]{4,3,2,1,0:T(8,128)(2,1)}, f32[512]{0:T(512)S(1)}, f32[512]{0:T(51...) while((s32[]{:T(128)}, ...), condition=%wide.region_15.16_spmd.clone, body=%wide.region_0.15_spmd.clone.sunk | while | flops 208999424 | bytes 16183717 | solution.py:174
  23.9 10.4 %all-to-all-start = ((f32[32,1,2048]{2,1,0:T(1,128)}), f32[32,1,2048]{2,1,0:T(1,128)S(1)}, u32[]{:S(2)}, u32[]{:S(2)}) async-start(f32[32,1,2048]{2,1,0:T(1,128)} %broadcast_in_dim.81), calls=%async_computation | async-start | bytes 524288 | tf_op jit(solution)/shard_map/while/body/eval_jaxpr/all_to_all | solution.py:11
  36.3 7.0 all-to-all-done
  92.2 7.0 all-to-all-done
  120.1 7.0 all-to-all-done
  148.1 7.0 all-to-all-done
  161.0 7.0 collective-permute-done
  177.3 7.0 all-to-all-done
  190.2 7.0 collective-permute-done
  219.3 7.0 collective-permute-done
  248.5 7.0 collective-permute-done
  277.7 7.0 collective-permute-done
  306.8 7.0 collective-permute-done
  336.0 7.0 collective-permute-done
  365.1 7.0 collective-permute-done
  394.3 7.0 collective-permute-done
  423.4 7.0 collective-permute-done
  452.6 7.0 collective-permute-done
  481.7 7.0 collective-permute-done
  510.9 7.0 collective-permute-done
  540.0 7.0 collective-permute-done
  569.2 7.0 collective-permute-done
  577.1 23.8 %all-gather = bf16[96,3,512]{2,1,0:T(4,128)(2,1)S(1)} all-gather(bf16[3,3,512]{2,1,0:T(4,128)(2,1)S(1)} %convert_element_type.113), channel_id=2, replica_groups=mesh['section'=16,'dp'=32] {'dp'}, dimensions={0}, use_global_device_ids=true | all-gather | bytes 304128 | tf_op jit(solution)/shard_map/all_gather | solution.py:178
  601.7 112.9 %all-reduce.5.cloned.1.call-done = bf16[1,512,512]{2,1,0:T(8,128)(2,1)} async-done(((bf16[1,512,512]{2,1,0:T(8,128)(2,1)}), bf16[1,512,512]{2,1,0:T(8,128)(2,1)}) %all-reduce.5.cloned.1.call-update) | async-done | bytes 524304 | tf_op jit(solution)/shard_map/psum | solution.py:177
  (506 shorter events, 420.9 us)
Async XLA Ops:
  7.2 707.4 %all-reduce.5.cloned.1.call-start = ((), (), s32[]{:S(2)}) async-start(), calls=%async_computation.1 | async-start | bytes 1048576 | tf_op jit(solution)/shard_map/psum | solution.py:177
  23.9 19.3 %all-to-all-start = ((f32[32,1,2048]{2,1,0:T(1,128)}), f32[32,1,2048]{2,1,0:T(1,128)S(1)}, u32[]{:S(2)}, u32[]{:S(2)}) async-start(f32[32,1,2048]{2,1,0:T(1,128)} %broadcast_in_dim.81), calls=%async_computation | async-start | bytes 524288 | tf_op jit(solution)/shard_map/while/body/eval_jaxpr/all_to_all | solution.py:11
  57.7 13.5 %all-to-all-start = ((f32[32,1,2048]{2,1,0:T(1,128)}), f32[32,1,2048]{2,1,0:T(1,128)S(1)}, u32[]{:S(2)}, u32[]{:S(2)}) async-start(f32[32,1,2048]{2,1,0:T(1,128)} %broadcast_in_dim.81), calls=%async_computation | async-start | bytes 524288 | tf_op jit(solution)/shard_map/while/body/eval_jaxpr/all_to_all | solution.py:11
  85.6 13.5 %all-to-all-start = ((f32[32,1,2048]{2,1,0:T(1,128)}), f32[32,1,2048]{2,1,0:T(1,128)S(1)}, u32[]{:S(2)}, u32[]{:S(2)}) async-start(f32[32,1,2048]{2,1,0:T(1,128)} %broadcast_in_dim.81), calls=%async_computation | async-start | bytes 524288 | tf_op jit(solution)/shard_map/while/body/eval_jaxpr/all_to_all | solution.py:11
  113.6 13.5 %all-to-all-start = ((f32[32,1,2048]{2,1,0:T(1,128)}), f32[32,1,2048]{2,1,0:T(1,128)S(1)}, u32[]{:S(2)}, u32[]{:S(2)}) async-start(f32[32,1,2048]{2,1,0:T(1,128)} %broadcast_in_dim.81), calls=%async_computation | async-start | bytes 524288 | tf_op jit(solution)/shard_map/while/body/eval_jaxpr/all_to_all | solution.py:11
  141.6 13.5 %all-to-all-start = ((f32[32,1,2048]{2,1,0:T(1,128)}), f32[32,1,2048]{2,1,0:T(1,128)S(1)}, u32[]{:S(2)}, u32[]{:S(2)}) async-start(f32[32,1,2048]{2,1,0:T(1,128)} %broadcast_in_dim.81), calls=%async_computation | async-start | bytes 524288 | tf_op jit(solution)/shard_map/while/body/eval_jaxpr/all_to_all | solution.py:11
  158.2 9.8 %collective-permute-start = (bf16[1,12,16,512]{3,2,1,0:T(8,128)(2,1)S(1)}, bf16[1,12,16,512]{3,2,1,0:T(8,128)(2,1)S(1)}, u32[]{:S(2)}, u32[]{:S(2)}) collective-permute-start(bf16[1,12,16,512]{3,2,1,0:T(8,128)(2,1)S(1)} %get-tuple-element.682), channel_id=1, source_target_pairs={{32,0},{64,32},{96,64},{128,96},{160,128},{192,160},{224,192},{256... | collective-permute-start | bytes 589832 | tf_op jit(solution)/shard_map/while/body/eval_jaxpr/ppermute | solution.py:31
  171.0 13.2 %all-to-all-start = ((f32[32,1,2048]{2,1,0:T(1,128)}), f32[32,1,2048]{2,1,0:T(1,128)S(1)}, u32[]{:S(2)}, u32[]{:S(2)}) async-start(f32[32,1,2048]{2,1,0:T(1,128)} %broadcast_in_dim.81), calls=%async_computation | async-start | bytes 524288 | tf_op jit(solution)/shard_map/while/body/eval_jaxpr/all_to_all | solution.py:11
  187.3 9.8 %collective-permute-start = (bf16[1,12,16,512]{3,2,1,0:T(8,128)(2,1)S(1)}, bf16[1,12,16,512]{3,2,1,0:T(8,128)(2,1)S(1)}, u32[]{:S(2)}, u32[]{:S(2)}) collective-permute-start(bf16[1,12,16,512]{3,2,1,0:T(8,128)(2,1)S(1)} %get-tuple-element.682), channel_id=1, source_target_pairs={{32,0},{64,32},{96,64},{128,96},{160,128},{192,160},{224,192},{256... | collective-permute-start | bytes 589832 | tf_op jit(solution)/shard_map/while/body/eval_jaxpr/ppermute | solution.py:31
  200.2 13.2 %all-to-all-start = ((f32[32,1,2048]{2,1,0:T(1,128)}), f32[32,1,2048]{2,1,0:T(1,128)S(1)}, u32[]{:S(2)}, u32[]{:S(2)}) async-start(f32[32,1,2048]{2,1,0:T(1,128)} %broadcast_in_dim.81), calls=%async_computation | async-start | bytes 524288 | tf_op jit(solution)/shard_map/while/body/eval_jaxpr/all_to_all | solution.py:11
  229.3 13.2 %all-to-all-start = ((f32[32,1,2048]{2,1,0:T(1,128)}), f32[32,1,2048]{2,1,0:T(1,128)S(1)}, u32[]{:S(2)}, u32[]{:S(2)}) async-start(f32[32,1,2048]{2,1,0:T(1,128)} %broadcast_in_dim.81), calls=%async_computation | async-start | bytes 524288 | tf_op jit(solution)/shard_map/while/body/eval_jaxpr/all_to_all | solution.py:11
  245.7 9.8 %collective-permute-start = (bf16[1,12,16,512]{3,2,1,0:T(8,128)(2,1)S(1)}, bf16[1,12,16,512]{3,2,1,0:T(8,128)(2,1)S(1)}, u32[]{:S(2)}, u32[]{:S(2)}) collective-permute-start(bf16[1,12,16,512]{3,2,1,0:T(8,128)(2,1)S(1)} %get-tuple-element.682), channel_id=1, source_target_pairs={{32,0},{64,32},{96,64},{128,96},{160,128},{192,160},{224,192},{256... | collective-permute-start | bytes 589832 | tf_op jit(solution)/shard_map/while/body/eval_jaxpr/ppermute | solution.py:31
  258.5 13.2 %all-to-all-start = ((f32[32,1,2048]{2,1,0:T(1,128)}), f32[32,1,2048]{2,1,0:T(1,128)S(1)}, u32[]{:S(2)}, u32[]{:S(2)}) async-start(f32[32,1,2048]{2,1,0:T(1,128)} %broadcast_in_dim.81), calls=%async_computation | async-start | bytes 524288 | tf_op jit(solution)/shard_map/while/body/eval_jaxpr/all_to_all | solution.py:11
  274.8 9.8 %collective-permute-start = (bf16[1,12,16,512]{3,2,1,0:T(8,128)(2,1)S(1)}, bf16[1,12,16,512]{3,2,1,0:T(8,128)(2,1)S(1)}, u32[]{:S(2)}, u32[]{:S(2)}) collective-permute-start(bf16[1,12,16,512]{3,2,1,0:T(8,128)(2,1)S(1)} %get-tuple-element.682), channel_id=1, source_target_pairs={{32,0},{64,32},{96,64},{128,96},{160,128},{192,160},{224,192},{256... | collective-permute-start | bytes 589832 | tf_op jit(solution)/shard_map/while/body/eval_jaxpr/ppermute | solution.py:31
  287.6 13.2 %all-to-all-start = ((f32[32,1,2048]{2,1,0:T(1,128)}), f32[32,1,2048]{2,1,0:T(1,128)S(1)}, u32[]{:S(2)}, u32[]{:S(2)}) async-start(f32[32,1,2048]{2,1,0:T(1,128)} %broadcast_in_dim.81), calls=%async_computation | async-start | bytes 524288 | tf_op jit(solution)/shard_map/while/body/eval_jaxpr/all_to_all | solution.py:11
  316.8 13.2 %all-to-all-start = ((f32[32,1,2048]{2,1,0:T(1,128)}), f32[32,1,2048]{2,1,0:T(1,128)S(1)}, u32[]{:S(2)}, u32[]{:S(2)}) async-start(f32[32,1,2048]{2,1,0:T(1,128)} %broadcast_in_dim.81), calls=%async_computation | async-start | bytes 524288 | tf_op jit(solution)/shard_map/while/body/eval_jaxpr/all_to_all | solution.py:11
  345.9 13.2 %all-to-all-start = ((f32[32,1,2048]{2,1,0:T(1,128)}), f32[32,1,2048]{2,1,0:T(1,128)S(1)}, u32[]{:S(2)}, u32[]{:S(2)}) async-start(f32[32,1,2048]{2,1,0:T(1,128)} %broadcast_in_dim.81), calls=%async_computation | async-start | bytes 524288 | tf_op jit(solution)/shard_map/while/body/eval_jaxpr/all_to_all | solution.py:11
  375.1 13.2 %all-to-all-start = ((f32[32,1,2048]{2,1,0:T(1,128)}), f32[32,1,2048]{2,1,0:T(1,128)S(1)}, u32[]{:S(2)}, u32[]{:S(2)}) async-start(f32[32,1,2048]{2,1,0:T(1,128)} %broadcast_in_dim.81), calls=%async_computation | async-start | bytes 524288 | tf_op jit(solution)/shard_map/while/body/eval_jaxpr/all_to_all | solution.py:11
  404.3 13.2 %all-to-all-start = ((f32[32,1,2048]{2,1,0:T(1,128)}), f32[32,1,2048]{2,1,0:T(1,128)S(1)}, u32[]{:S(2)}, u32[]{:S(2)}) async-start(f32[32,1,2048]{2,1,0:T(1,128)} %broadcast_in_dim.81), calls=%async_computation | async-start | bytes 524288 | tf_op jit(solution)/shard_map/while/body/eval_jaxpr/all_to_all | solution.py:11
  433.4 13.2 %all-to-all-start = ((f32[32,1,2048]{2,1,0:T(1,128)}), f32[32,1,2048]{2,1,0:T(1,128)S(1)}, u32[]{:S(2)}, u32[]{:S(2)}) async-start(f32[32,1,2048]{2,1,0:T(1,128)} %broadcast_in_dim.81), calls=%async_computation | async-start | bytes 524288 | tf_op jit(solution)/shard_map/while/body/eval_jaxpr/all_to_all | solution.py:11
  462.6 13.2 %all-to-all-start = ((f32[32,1,2048]{2,1,0:T(1,128)}), f32[32,1,2048]{2,1,0:T(1,128)S(1)}, u32[]{:S(2)}, u32[]{:S(2)}) async-start(f32[32,1,2048]{2,1,0:T(1,128)} %broadcast_in_dim.81), calls=%async_computation | async-start | bytes 524288 | tf_op jit(solution)/shard_map/while/body/eval_jaxpr/all_to_all | solution.py:11
  491.7 13.2 %all-to-all-start = ((f32[32,1,2048]{2,1,0:T(1,128)}), f32[32,1,2048]{2,1,0:T(1,128)S(1)}, u32[]{:S(2)}, u32[]{:S(2)}) async-start(f32[32,1,2048]{2,1,0:T(1,128)} %broadcast_in_dim.81), calls=%async_computation | async-start | bytes 524288 | tf_op jit(solution)/shard_map/while/body/eval_jaxpr/all_to_all | solution.py:11
  520.9 13.2 %all-to-all-start = ((f32[32,1,2048]{2,1,0:T(1,128)}), f32[32,1,2048]{2,1,0:T(1,128)S(1)}, u32[]{:S(2)}, u32[]{:S(2)}) async-start(f32[32,1,2048]{2,1,0:T(1,128)} %broadcast_in_dim.81), calls=%async_computation | async-start | bytes 524288 | tf_op jit(solution)/shard_map/while/body/eval_jaxpr/all_to_all | solution.py:11
  550.0 13.2 %all-to-all-start = ((f32[32,1,2048]{2,1,0:T(1,128)}), f32[32,1,2048]{2,1,0:T(1,128)S(1)}, u32[]{:S(2)}, u32[]{:S(2)}) async-start(f32[32,1,2048]{2,1,0:T(1,128)} %broadcast_in_dim.81), calls=%async_computation | async-start | bytes 524288 | tf_op jit(solution)/shard_map/while/body/eval_jaxpr/all_to_all | solution.py:11
  (41 other events, 619.8 us)
Sparse Core Ops, SparseCore 0:
  577.2 137.3 all-reduce.4
